TPU v7x, 32 devices: a whole 2x2x4 slice. The times are simulated.
32 devices in a mesh: grp: 2 (over y), gx: 16 (over z, x, core), gy: 1.
Axes of the slice: x: 2, y: 2, z: 4, core: 2. Of those that a mesh axis runs over, the one named last changes fastest.
Arguments:
- residue_feats: bfloat16 [512, 256], P(('grp', 'gx')), parts along dimension 0, may hold values from -6 to 6
- pair_feats: bfloat16 [64, 512, 256], P(None, ('grp', 'gx'), 'gy'), parts along dimension 1, may hold values from -30 to 30
- w_row: bfloat16 [256, 64], replicated, may hold values from -0.375 to 0.375
- w_col: bfloat16 [256, 64], replicated, may hold values from -0.375 to 0.375
- first_taps: bfloat16 [9, 64, 64], replicated, may hold values from -0.25 to 0.25
- second_taps: bfloat16 [9, 64, 64], replicated, may hold values from -0.25 to 0.25
- norm_scale: float32 [2, 64], replicated, may hold values from 0.25 to 1.75
- norm_shift: float32 [2, 64], replicated, may hold values from -2 to 2
Outputs:
- symmetric: bfloat16 [64, 512, 256], P(None, ('grp', 'gx'), 'gy'), parts along dimension 1
There are 2 independent parts, one for each index of `grp`. A program takes and returns all parts, laid end to end along the dimension named above; an argument that names none is the same for every part. Nothing has to cross between parts.
All inputs are finite; a program needn't handle non-finite values.
Results may differ from a plain program's by a relative error of at most 0.012.
Values may be sent and summed in bfloat16 or wider, within the bound.
A program may use at most 64 MiB of HBM per device.

v0:
```python
import jax
import jax.numpy as jnp
from jax import lax
from jax.sharding import PartitionSpec as P

DILATION_STEP = 8
epsilon = 1e-05


def with_halo(cells, sides, width):
    for axis, dim in sides:
        count = lax.axis_size(axis)
        ends = count - 1
        head = lax.slice_in_dim(cells, 0, width, axis=dim)
        tail = lax.slice_in_dim(cells, cells.shape[dim] - width, cells.shape[dim], axis=dim)
        cells = jnp.concatenate(
            [
                lax.ppermute(tail, axis, [(i, (i + 1) % count) for i in range(ends)]),
                cells,
                lax.ppermute(head, axis, [((i + 1) % count, i) for i in range(ends)]),
            ],
            axis=dim,
        )
    return cells


def dilated(receptive_region, weights):
    row_count = receptive_region.shape[1]
    col_count = receptive_region.shape[2]
    border_padded_input = with_halo(receptive_region, (("gx", 1), ("gy", 2)), DILATION_STEP)
    tap_sum_total = jnp.zeros((weights.shape[1], row_count, col_count), jnp.float32)
    for filter_tap_index in range(9):
        row_displacement = filter_tap_index // 3 * DILATION_STEP
        column_displacement = filter_tap_index % 3 * DILATION_STEP
        window = border_padded_input[
            :,
            row_displacement : row_displacement + row_count,
            column_displacement : column_displacement + col_count,
        ]
        tap_sum_total = tap_sum_total + jnp.einsum(
            "oc,crw->orw", weights[filter_tap_index], window, preferred_element_type=jnp.float32
        )
    return tap_sum_total


def normalized(tap_sum_total, gain, shift):
    cell_count = (
        tap_sum_total.shape[1] * tap_sum_total.shape[2] * lax.axis_size("gx") * lax.axis_size("gy")
    )
    first_sum, second_sum = lax.psum(
        (jnp.sum(tap_sum_total, axis=(1, 2)), jnp.sum(tap_sum_total * tap_sum_total, axis=(1, 2))),
        ("gx", "gy"),
    )
    average = first_sum / cell_count
    spread = second_sum / cell_count - average * average
    centred = tap_sum_total - average[:, None, None]
    factor = gain * lax.rsqrt(spread + epsilon)
    return centred * factor[:, None, None] + shift[:, None, None]


def body(residue_feats, pair_feats, w_row, w_col, first_taps, second_taps, norm_scale, norm_shift):
    col_count = pair_feats.shape[2]
    col_start = lax.axis_index("gy") * col_count
    row_part = jnp.dot(residue_feats, w_row, preferred_element_type=jnp.float32).astype(
        jnp.bfloat16
    )
    everyone = lax.all_gather(residue_feats, "gx", axis=0, tiled=True)
    col_feats = lax.dynamic_slice_in_dim(everyone, col_start, col_count, 0)
    col_part = jnp.dot(col_feats, w_col, preferred_element_type=jnp.float32).astype(jnp.bfloat16)
    block_in = (
        pair_feats.astype(jnp.float32)
        + row_part.T.astype(jnp.float32)[:, :, None]
        + col_part.T.astype(jnp.float32)[:, None, :]
    ).astype(jnp.bfloat16)
    first_conv = dilated(block_in, first_taps)
    activated = jax.nn.elu(normalized(first_conv, norm_scale[0], norm_shift[0])).astype(
        jnp.bfloat16
    )
    second_conv = dilated(activated, second_taps)
    block_out = jax.nn.elu(
        block_in.astype(jnp.float32) + normalized(second_conv, norm_scale[1], norm_shift[1])
    ).astype(jnp.bfloat16)
    whole_rows = lax.all_gather(block_out, "gy", axis=2, tiled=True)
    columns = lax.all_to_all(whole_rows, "gx", split_axis=2, concat_axis=1, tiled=True)
    flipped = lax.dynamic_slice_in_dim(columns, col_start, col_count, 1)
    mirrored = jnp.transpose(flipped, (0, 2, 1))
    return (0.5 * (block_out.astype(jnp.float32) + mirrored.astype(jnp.float32))).astype(
        jnp.bfloat16
    )


def solution(mesh):
    placed = (P(("grp", "gx"), None), P(None, ("grp", "gx"), "gy"), P(), P(), P(), P(), P(), P())
    return jax.shard_map(
        body, mesh=mesh, in_specs=placed, out_specs=P(None, ("grp", "gx"), "gy"), check_vma=False
    )
```

profile of v0, /device:TPU:0, one launch (start us, length us, event | category | flops | bytes accessed | tf_op | source)
XLA Modules:
  0.0 140.1 jit_solution(18333366935052121485)
XLA Ops:
  0.0 23.8 %all_gather.4 = bf16[256,256]{1,0:T(8,128)(2,1)S(1)} all-gather(bf16[16,256]{1,0:T(8,128)(2,1)} %param.8), channel_id=1, replica_groups=mesh['grp'=2,'gx'=16,'gy'=1] {'gx'}, dimensions={0}, use_global_device_ids=true | all-gather | bytes 139264 | tf_op jit(solution)/shard_map/all_gather | solution.py:67
  23.8 0.9 fusion.13
  24.9 1.3 add_convert_fusion
  26.2 2.3 %collective-permute-start = (bf16[64,8,256]{2,0,1:T(8,128)(2,1)S(1)}, bf16[64,8,256]{2,0,1:T(8,128)(2,1)S(1)}, u32[]{:S(2)}, u32[]{:S(2)}) collective-permute-start(bf16[64,8,256]{2,0,1:T(8,128)(2,1)S(1)} %get-tuple-element.23), channel_id=1, source_target_pairs={{0,1},{1,2},{2,3},{3,4},{4,5},{5,6},{6,7},{7,8},{8,9},{9,10},{10,1... | collective-permute-start | bytes 786440 | tf_op jit(solution)/shard_map/ppermute | solution.py:18
  28.5 1.3 collective-permute-start.1
  30.1 1.8 %collective-permute-done.1 = bf16[64,8,256]{2,0,1:T(8,128)(2,1)S(1)} collective-permute-done((bf16[64,8,256]{2,0,1:T(8,128)(2,1)S(1)}, bf16[64,8,256]{2,0,1:T(8,128)(2,1)S(1)}, u32[]{:S(2)}, u32[]{:S(2)}) %collective-permute-start.1) | collective-permute-done | bytes 262176 | tf_op jit(solution)/shard_map/ppermute | solution.py:20
  32.3 0.7 collective-permute-start.2
  33.0 0.7 collective-permute-start.3
  34.3 1.3 maximum_maximum_fusion
  38.0 33.9 %all-reduce.1 = (f32[64]{0:T(128)S(1)}, f32[64]{0:T(128)S(1)}) all-reduce(f32[64]{0:T(128)S(1)} %get-tuple-element.8, f32[64]{0:T(128)S(1)} %get-tuple-element.7), channel_id=1, replica_groups=mesh['grp'=2,'gx'=16,'gy'=1] {'gx','gy'}, use_global_device_ids=true, to_apply=%region_3.0 | all-reduce | flops 128 | bytes 1024 | tf_op jit(solution)/shard_map/psum | solution.py:50
  72.6 1.3 collective-permute-start.4
  73.9 1.3 collective-permute-start.5
  75.5 1.8 %collective-permute-done.5 = bf16[64,8,256]{2,0,1:T(8,128)(2,1)S(1)} collective-permute-done((bf16[64,8,256]{2,0,1:T(8,128)(2,1)S(1)}, bf16[64,8,256]{2,0,1:T(8,128)(2,1)S(1)}, u32[]{:S(2)}, u32[]{:S(2)}) %collective-permute-start.5) | collective-permute-done | bytes 262176 | tf_op jit(solution)/shard_map/ppermute | solution.py:20
  77.8 0.7 collective-permute-start.6
  78.5 0.7 collective-permute-start.7
  79.7 1.3 maximum_maximum_fusion.1
  83.4 31.5 %all-reduce = (f32[64]{0:T(128)S(1)}, f32[64]{0:T(128)S(1)}) all-reduce(f32[64]{0:T(128)S(1)} %get-tuple-element.6, f32[64]{0:T(128)S(1)} %get-tuple-element.5), channel_id=1, replica_groups=mesh['grp'=2,'gx'=16,'gy'=1] {'gx','gy'}, use_global_device_ids=true, to_apply=%region_7.8 | all-reduce | flops 128 | bytes 1024 | tf_op jit(solution)/shard_map/psum | solution.py:50
  115.0 0.7 fusion.17
  115.7 1.0 copy.18
  116.7 0.7 reshape.32
  117.4 16.9 %all_to_all.4 = bf16[16,2,8192]{2,1,0:T(2,128)(2,1)S(1)} all-to-all(bf16[16,2,8192]{2,1,0:T(2,128)(2,1)S(1)} %reshape.32), channel_id=1, replica_groups=mesh['grp'=2,'gx'=16,'gy'=1] {'gx'}, dimensions={0} | all-to-all | bytes 1048576 | tf_op jit(solution)/shard_map/all_to_all | solution.py:84
  135.7 2.0 %copy.21 = f32[64,256,16]{1,0,2:T(8,128)} copy(f32[64,256,16]{0,2,1:T(8,128)S(1)} %bitcast.109) | data formatting | bytes 2097152 | tf_op jit(solution)/shard_map/convert_element_type | solution.py:87
  137.6 1.4 fusion.19
  139.0 1.1 copy.22
  (51 shorter events, 9.4 us)
Async XLA Ops:
  0.0 24.7 %copy-start = (bf16[256,64]{0,1:T(8,128)(2,1)S(1)}, bf16[256,64]{0,1:T(8,128)(2,1)}, u32[]{:S(2)}) copy-start(bf16[256,64]{0,1:T(8,128)(2,1)} %param.11) | copy-start | bytes 98308
  0.0 29.8 %copy-start.5 = (f32[2,64]{1,0:T(2,128)S(1)}, f32[2,64]{1,0:T(2,128)}, u32[]{:S(2)}) copy-start(f32[2,64]{1,0:T(2,128)} %param.15) | copy-start | bytes 1540
  0.0 29.8 %copy-start.2 = (bf16[9,64,64]{2,1,0:T(8,128)(2,1)S(1)}, bf16[9,64,64]{2,1,0:T(8,128)(2,1)}, u32[]{:S(2)}) copy-start(bf16[9,64,64]{2,1,0:T(8,128)(2,1)} %param.12) | copy-start | bytes 221188
  26.2 3.9 %collective-permute-start = (bf16[64,8,256]{2,0,1:T(8,128)(2,1)S(1)}, bf16[64,8,256]{2,0,1:T(8,128)(2,1)S(1)}, u32[]{:S(2)}, u32[]{:S(2)}) collective-permute-start(bf16[64,8,256]{2,0,1:T(8,128)(2,1)S(1)} %get-tuple-element.23), channel_id=1, source_target_pairs={{0,1},{1,2},{2,3},{3,4},{4,5},{5,6},{6,7},{7,8},{8,9},{9,10},{10,1... | collective-permute-start | bytes 786440 | tf_op jit(solution)/shard_map/ppermute | solution.py:18
  28.5 3.4 %collective-permute-start.1 = (bf16[64,8,256]{2,0,1:T(8,128)(2,1)S(1)}, bf16[64,8,256]{2,0,1:T(8,128)(2,1)S(1)}, u32[]{:S(2)}, u32[]{:S(2)}) collective-permute-start(bf16[64,8,256]{2,0,1:T(8,128)(2,1)S(1)} %get-tuple-element.24), channel_id=1, source_target_pairs={{1,0},{2,1},{3,2},{4,3},{5,4},{6,5},{7,6},{8,7},{9,8},{10,9},{11,1... | collective-permute-start | bytes 786440 | tf_op jit(solution)/shard_map/ppermute | solution.py:20
  32.3 1.9 %collective-permute-start.2 = (bf16[64,32,8]{2,0,1:T(8,128)(2,1)S(1)}, bf16[64,32,8]{2,0,1:T(8,128)(2,1)S(1)}, u32[]{:S(2)}, u32[]{:S(2)}) collective-permute-start(bf16[64,32,8]{2,0,1:T(8,128)(2,1)S(1)} %get-tuple-element.19), channel_id=1, source_target_pairs={} | collective-permute-start | bytes 98312 | tf_op jit(solution)/shard_map/ppermute | solution.py:18
  33.0 1.3 collective-permute-start.3
  37.3 34.6 %copy-start.4 = (f32[2,64]{1,0:T(2,128)S(1)}, f32[2,64]{1,0:T(2,128)}, u32[]{:S(2)}) copy-start(f32[2,64]{1,0:T(2,128)} %param.14) | copy-start | bytes 1540
  38.0 37.2 %copy-start.3 = (bf16[9,64,64]{2,1,0:T(8,128)(2,1)S(1)}, bf16[9,64,64]{2,1,0:T(8,128)(2,1)}, u32[]{:S(2)}) copy-start(bf16[9,64,64]{2,1,0:T(8,128)(2,1)} %param.13) | copy-start | bytes 221188
  72.6 2.9 %collective-permute-start.4 = (bf16[64,8,256]{2,0,1:T(8,128)(2,1)S(1)}, bf16[64,8,256]{2,0,1:T(8,128)(2,1)S(1)}, u32[]{:S(2)}, u32[]{:S(2)}) collective-permute-start(bf16[64,8,256]{2,0,1:T(8,128)(2,1)S(1)} %get-tuple-element.21), channel_id=1, source_target_pairs={{0,1},{1,2},{2,3},{3,4},{4,5},{5,6},{6,7},{7,8},{8,9},{9,10},{10,1... | collective-permute-start | bytes 786440 | tf_op jit(solution)/shard_map/ppermute | solution.py:18
  73.9 3.4 %collective-permute-start.5 = (bf16[64,8,256]{2,0,1:T(8,128)(2,1)S(1)}, bf16[64,8,256]{2,0,1:T(8,128)(2,1)S(1)}, u32[]{:S(2)}, u32[]{:S(2)}) collective-permute-start(bf16[64,8,256]{2,0,1:T(8,128)(2,1)S(1)} %get-tuple-element.22), channel_id=1, source_target_pairs={{1,0},{2,1},{3,2},{4,3},{5,4},{6,5},{7,6},{8,7},{9,8},{10,9},{11,1... | collective-permute-start | bytes 786440 | tf_op jit(solution)/shard_map/ppermute | solution.py:20
  77.8 1.9 %collective-permute-start.6 = (bf16[64,32,8]{2,0,1:T(8,128)(2,1)S(1)}, bf16[64,32,8]{2,0,1:T(8,128)(2,1)S(1)}, u32[]{:S(2)}, u32[]{:S(2)}) collective-permute-start(bf16[64,32,8]{2,0,1:T(8,128)(2,1)S(1)} %get-tuple-element.15), channel_id=1, source_target_pairs={} | collective-permute-start | bytes 98312 | tf_op jit(solution)/shard_map/ppermute | solution.py:18
  78.5 1.3 collective-permute-start.7
  82.7 32.2 %copy-start.1 = (bf16[64,16,256]{2,1,0:T(8,128)(2,1)S(1)}, bf16[64,16,256]{2,1,0:T(8,128)(2,1)}, u32[]{:S(2)}) copy-start(bf16[64,16,256]{2,1,0:T(8,128)(2,1)} %param.9) | copy-start | bytes 1572868
where the time goes:
time: 141 us; the launch traced here: 140 us
  blocking collectives  106 us (75%)
  starting transfers between devices  8.9 us (6%)
  matrix products  7.38 us (5%)
  other arithmetic  7.08 us (5%)
  local copies, waits for them, and re-layouts  6.52 us (5%)
  waiting for transfers between devices  3.66 us (3%)
    psum x2, blocking collectives, normalized(): lax.psum((jnp.sum(tap_sum_total, axis=(1, 2)), jnp.sum(tap_sum_total * ta...  65.5 us
    all_gather x1, blocking collectives, body(): everyone = lax.all_gather(residue_feats, 'gx', axis=0, tiled=True)  23.8 us
    all_to_all x1, blocking collectives, body(): lax.all_to_all(whole_rows, 'gx', split_axis=2, concat_axis=1, tiled=True)  16.9 us
    dot_general x18, matrix products, dilated(): jnp.einsum('oc,crw->orw', weights[filter_tap_index], window, preferred_el...  6.34 us
    ppermute x4, starting transfers between devices, with_halo(): lax.ppermute(tail, axis, [(i, (i + 1) % count) for i in range(ends)])  4.94 us
    ppermute x4, starting transfers between devices, with_halo(): lax.ppermute(head, axis, [((i + 1) % count, i) for i in range(ends)])  3.96 us
    ppermute x4, waiting for transfers between devices, with_halo(): lax.ppermute(head, axis, [((i + 1) % count, i) for i in range(ends)])  3.65 us
    concatenate x4, other arithmetic, with_halo(): jnp.concatenate([lax.ppermute(tail, axis, [(i, (i + 1) % count) for i in...  2.87 us
  transfers between devices with their start and end apart: 8, of which 2 were waited for; matrix products, arithmetic and copies ran while one was open for 1% of the time, Pallas kernels for 0%

commit v1 on v0

--- a/solution.py
+++ b/solution.py
@@ -5,6 +5,24 @@
 
 DILATION_STEP = 8
 epsilon = 1e-05
+
+
+def laid_out(tiles, dim):
+    tiles = jnp.moveaxis(tiles, 0, dim)
+    lengths = tiles.shape
+    return tiles.reshape(*lengths[:dim], lengths[dim] * lengths[dim + 1], *lengths[dim + 2 :])
+
+
+def grow_blocks(shard, axis):
+    length = lax.axis_size(axis)
+    blocks = shard[None]
+    for level in range(length.bit_length() - 1):
+        apart = 1 << level
+        partner_block = lax.ppermute(blocks, axis, [(i, i ^ apart) for i in range(length)])
+        both = jnp.stack([blocks, partner_block])
+        upper = lax.axis_index(axis) >> level & 1
+        blocks = jnp.where(upper == 0, both, both[::-1]).reshape(-1, *shard.shape)
+    return blocks
 
 
 def with_halo(cells, sides, width):
@@ -64,7 +82,7 @@
     row_part = jnp.dot(residue_feats, w_row, preferred_element_type=jnp.float32).astype(
         jnp.bfloat16
     )
-    everyone = lax.all_gather(residue_feats, "gx", axis=0, tiled=True)
+    everyone = laid_out(grow_blocks(residue_feats, "gx"), 0)
     col_feats = lax.dynamic_slice_in_dim(everyone, col_start, col_count, 0)
     col_part = jnp.dot(col_feats, w_col, preferred_element_type=jnp.float32).astype(jnp.bfloat16)
     block_in = (

time: 141 us -> 135 us (0.957)
  blocking collectives: 106 us -> 84.7 us
  starting transfers between devices: 8.9 us -> 16.6 us
  waiting for transfers between devices: 3.66 us -> 11 us
    all_gather x1 -> x0, blocking collectives: 23.8 us -> none  [body(): everyone = lax.all_gather(residue_feats, 'gx', axis=0, tiled=True)]
    ppermute x0 -> x4, starting transfers between devices: none -> 8.64 us  [grow_blocks(): lax.ppermute(blocks, axis, [(i, i ^ apart) for i in range(length)])]
    ppermute x0 -> x4, waiting for transfers between devices: none -> 5.26 us  [grow_blocks(): lax.ppermute(blocks, axis, [(i, i ^ apart) for i in range(length)])]
    psum x2, blocking collectives: 65.5 us -> 67.6 us  [normalized(): lax.psum((jnp.sum(tap_sum_total, axis=(1, 2)), jnp.sum(tap_sum_total * ta...]
    ppermute x4, waiting for transfers between devices: 3.65 us -> 5.7 us  [with_halo(): lax.ppermute(head, axis, [((i + 1) % count, i) for i in range(ends)])]
  transfers between devices with their start and end apart: 8 -> 12, of which waited for: 2 -> 6; matrix products, arithmetic and copies ran while one was open for 1% -> 2% of each run, Pallas kernels for 0% -> 0%
where the time goes in v1:
time: 135 us; the launch traced here: 134 us
  blocking collectives  84.7 us (63%)
  starting transfers between devices  16.6 us (12%)
  waiting for transfers between devices  11 us (8%)
  matrix products  7.39 us (5%)
  local copies, waits for them, and re-layouts  7.27 us (5%)
  other arithmetic  6.84 us (5%)
    psum x2, blocking collectives, normalized(): lax.psum((jnp.sum(tap_sum_total, axis=(1, 2)), jnp.sum(tap_sum_total * ta...  67.6 us
    all_to_all x1, blocking collectives, body(): lax.all_to_all(whole_rows, 'gx', split_axis=2, concat_axis=1, tiled=True)  17.1 us
    ppermute x4, starting transfers between devices, grow_blocks(): lax.ppermute(blocks, axis, [(i, i ^ apart) for i in range(length)])  8.64 us
    dot_general x18, matrix products, dilated(): jnp.einsum('oc,crw->orw', weights[filter_tap_index], window, preferred_el...  6.36 us
    ppermute x4, waiting for transfers between devices, with_halo(): lax.ppermute(head, axis, [((i + 1) % count, i) for i in range(ends)])  5.7 us
    ppermute x4, waiting for transfers between devices, grow_blocks(): lax.ppermute(blocks, axis, [(i, i ^ apart) for i in range(length)])  5.26 us
    ppermute x4, starting transfers between devices, with_halo(): lax.ppermute(tail, axis, [(i, (i + 1) % count) for i in range(ends)])  3.99 us
    ppermute x4, starting transfers between devices, with_halo(): lax.ppermute(head, axis, [((i + 1) % count, i) for i in range(ends)])  3.96 us
  transfers between devices with their start and end apart: 12, of which 6 were waited for; matrix products, arithmetic and copies ran while one was open for 2% of the time, Pallas kernels for 0%

profile of v1, /device:TPU:0, one launch (start us, length us, event | category | flops | bytes accessed | tf_op | source)
XLA Modules:
  0.0 134.1 jit_solution(10449684957209514085)
XLA Ops:
  0.5 1.0 collective-permute-done
  2.2 2.9 %collective-permute-start.1 = (bf16[2,16,256]{2,1,0:T(8,128)(2,1)S(1)}, bf16[2,16,256]{2,1,0:T(8,128)(2,1)S(1)}, u32[]{:S(2)}, u32[]{:S(2)}) collective-permute-start(bf16[2,16,256]{2,1,0:T(8,128)(2,1)S(1)} %get-tuple-element.26), channel_id=1, source_target_pairs={{0,2},{1,3},{2,0},{3,1},{4,6},{5,7},{6,4},{7,5},{8,10},{9,11},{10,... | collective-permute-start | bytes 49160 | tf_op jit(solution)/shard_map/ppermute | solution.py:21
  5.1 1.7 %collective-permute-done.1 = bf16[2,16,256]{2,1,0:T(8,128)(2,1)S(1)} collective-permute-done((bf16[2,16,256]{2,1,0:T(8,128)(2,1)S(1)}, bf16[2,16,256]{2,1,0:T(8,128)(2,1)S(1)}, u32[]{:S(2)}, u32[]{:S(2)}) %collective-permute-start.1) | collective-permute-done | bytes 16416 | tf_op jit(solution)/shard_map/ppermute | solution.py:21
  6.9 2.2 %collective-permute-start.2 = (bf16[4,16,256]{2,1,0:T(8,128)(2,1)S(1)}, bf16[4,16,256]{2,1,0:T(8,128)(2,1)S(1)}, u32[]{:S(2)}, u32[]{:S(2)}) collective-permute-start(bf16[4,16,256]{2,1,0:T(8,128)(2,1)S(1)} %bitcast.133), channel_id=1, source_target_pairs={{0,4},{1,5},{2,6},{3,7},{4,0},{5,1},{6,2},{7,3},{8,12},{9,13},{10,... | collective-permute-start | bytes 98312 | tf_op jit(solution)/shard_map/ppermute | solution.py:21
  9.0 0.9 fusion.14
  9.9 1.0 collective-permute-done.2
  11.0 3.1 %collective-permute-start.3 = (bf16[8,16,256]{2,1,0:T(8,128)(2,1)S(1)}, bf16[8,16,256]{2,1,0:T(8,128)(2,1)S(1)}, u32[]{:S(2)}, u32[]{:S(2)}) collective-permute-start(bf16[8,16,256]{2,1,0:T(8,128)(2,1)S(1)} %bitcast.131), channel_id=1, source_target_pairs={{0,8},{1,9},{2,10},{3,11},{4,12},{5,13},{6,14},{7,15},{8,0},{9,1},... | collective-permute-start | bytes 196616 | tf_op jit(solution)/shard_map/ppermute | solution.py:21
  14.1 0.8 slice_bitcast_fusion
  14.8 1.5 %collective-permute-done.3 = bf16[8,16,256]{2,1,0:T(8,128)(2,1)S(1)} collective-permute-done((bf16[8,16,256]{2,1,0:T(8,128)(2,1)S(1)}, bf16[8,16,256]{2,1,0:T(8,128)(2,1)S(1)}, u32[]{:S(2)}, u32[]{:S(2)}) %collective-permute-start.3) | collective-permute-done | bytes 65568 | tf_op jit(solution)/shard_map/ppermute | solution.py:21
  16.8 1.3 collective-permute-start.4
  18.2 1.3 collective-permute-start.5
  19.8 3.9 %collective-permute-done.5 = bf16[64,8,256]{2,0,1:T(8,128)(2,1)S(1)} collective-permute-done((bf16[64,8,256]{2,0,1:T(8,128)(2,1)S(1)}, bf16[64,8,256]{2,0,1:T(8,128)(2,1)S(1)}, u32[]{:S(2)}, u32[]{:S(2)}) %collective-permute-start.5) | collective-permute-done | bytes 262176 | tf_op jit(solution)/shard_map/ppermute | solution.py:38
  26.0 1.3 maximum_maximum_fusion
  29.7 34.7 %all-reduce.1 = (f32[64]{0:T(128)S(1)}, f32[64]{0:T(128)S(1)}) all-reduce(f32[64]{0:T(128)S(1)} %get-tuple-element.8, f32[64]{0:T(128)S(1)} %get-tuple-element.7), channel_id=1, replica_groups=mesh['grp'=2,'gx'=16,'gy'=1] {'gx','gy'}, use_global_device_ids=true, to_apply=%region_3.4 | all-reduce | flops 128 | bytes 1024 | tf_op jit(solution)/shard_map/psum | solution.py:68
  65.1 1.3 collective-permute-start.8
  66.4 1.3 collective-permute-start.9
  68.0 1.8 %collective-permute-done.9 = bf16[64,8,256]{2,0,1:T(8,128)(2,1)S(1)} collective-permute-done((bf16[64,8,256]{2,0,1:T(8,128)(2,1)S(1)}, bf16[64,8,256]{2,0,1:T(8,128)(2,1)S(1)}, u32[]{:S(2)}, u32[]{:S(2)}) %collective-permute-start.9) | collective-permute-done | bytes 262176 | tf_op jit(solution)/shard_map/ppermute | solution.py:38
  72.2 1.3 maximum_maximum_fusion.1
  75.9 33.0 %all-reduce = (f32[64]{0:T(128)S(1)}, f32[64]{0:T(128)S(1)}) all-reduce(f32[64]{0:T(128)S(1)} %get-tuple-element.6, f32[64]{0:T(128)S(1)} %get-tuple-element.5), channel_id=1, replica_groups=mesh['grp'=2,'gx'=16,'gy'=1] {'gx','gy'}, use_global_device_ids=true, to_apply=%region_7.8 | all-reduce | flops 128 | bytes 1024 | tf_op jit(solution)/shard_map/psum | solution.py:68
  109.6 1.0 copy.18
  111.3 17.1 %all_to_all.4 = bf16[16,2,8192]{2,1,0:T(2,128)(2,1)S(1)} all-to-all(bf16[16,2,8192]{2,1,0:T(2,128)(2,1)S(1)} %reshape.44), channel_id=1, replica_groups=mesh['grp'=2,'gx'=16,'gy'=1] {'gx'}, dimensions={0} | all-to-all | bytes 1048576 | tf_op jit(solution)/shard_map/all_to_all | solution.py:102
  129.7 2.0 %copy.21 = f32[64,256,16]{1,0,2:T(8,128)} copy(f32[64,256,16]{0,2,1:T(8,128)S(1)} %bitcast.126) | data formatting | bytes 2097152 | tf_op jit(solution)/shard_map/convert_element_type | solution.py:105
  131.7 1.4 %fusion.20 = bf16[64,16,256]{2,0,1:T(8,128)(2,1)S(1)} fusion(f32[64,256,16]{1,0,2:T(8,128)} %copy.21, bf16[64,16,256]{2,0,1:T(8,128)(2,1)S(1)} %fusion.18), kind=kLoop, calls=%fused_computation.38 | loop fusion | flops 1048576 | bytes 2097152 | tf_op jit(solution)/shard_map/convert_element_type | solution.py:105
  133.1 1.1 copy.22
  (64 shorter events, 15.1 us)
Async XLA Ops:
  0.0 16.4 %copy-start = (bf16[256,64]{0,1:T(8,128)(2,1)S(1)}, bf16[256,64]{0,1:T(8,128)(2,1)}, u32[]{:S(2)}) copy-start(bf16[256,64]{0,1:T(8,128)(2,1)} %param.11) | copy-start | bytes 98308
  0.0 16.5 %copy-start.1 = (bf16[64,16,256]{2,1,0:T(8,128)(2,1)S(1)}, bf16[64,16,256]{2,1,0:T(8,128)(2,1)}, u32[]{:S(2)}) copy-start(bf16[64,16,256]{2,1,0:T(8,128)(2,1)} %param.9) | copy-start | bytes 1572868
  0.0 1.5 %collective-permute-start = (bf16[1,16,256]{2,1,0:T(8,128)(2,1)}, bf16[1,16,256]{2,1,0:T(8,128)(2,1)S(1)}, u32[]{:S(2)}, u32[]{:S(2)}) collective-permute-start(bf16[1,16,256]{2,1,0:T(8,128)(2,1)} %bitcast.137), channel_id=1, source_target_pairs={{0,1},{1,0},{2,3},{3,2},{4,5},{5,4},{6,7},{7,6},{8,9},{9,8},{10,11... | collective-permute-start | bytes 24584 | tf_op jit(solution)/shard_map/ppermute | solution.py:21
  2.2 4.6 %collective-permute-start.1 = (bf16[2,16,256]{2,1,0:T(8,128)(2,1)S(1)}, bf16[2,16,256]{2,1,0:T(8,128)(2,1)S(1)}, u32[]{:S(2)}, u32[]{:S(2)}) collective-permute-start(bf16[2,16,256]{2,1,0:T(8,128)(2,1)S(1)} %get-tuple-element.26), channel_id=1, source_target_pairs={{0,2},{1,3},{2,0},{3,1},{4,6},{5,7},{6,4},{7,5},{8,10},{9,11},{10,... | collective-permute-start | bytes 49160 | tf_op jit(solution)/shard_map/ppermute | solution.py:21
  6.9 4.1 %collective-permute-start.2 = (bf16[4,16,256]{2,1,0:T(8,128)(2,1)S(1)}, bf16[4,16,256]{2,1,0:T(8,128)(2,1)S(1)}, u32[]{:S(2)}, u32[]{:S(2)}) collective-permute-start(bf16[4,16,256]{2,1,0:T(8,128)(2,1)S(1)} %bitcast.133), channel_id=1, source_target_pairs={{0,4},{1,5},{2,6},{3,7},{4,0},{5,1},{6,2},{7,3},{8,12},{9,13},{10,... | collective-permute-start | bytes 98312 | tf_op jit(solution)/shard_map/ppermute | solution.py:21
  10.9 8.5 %copy-start.2 = (bf16[9,64,64]{2,1,0:T(8,128)(2,1)S(1)}, bf16[9,64,64]{2,1,0:T(8,128)(2,1)}, u32[]{:S(2)}) copy-start(bf16[9,64,64]{2,1,0:T(8,128)(2,1)} %param.12) | copy-start | bytes 221188
  11.0 5.3 %collective-permute-start.3 = (bf16[8,16,256]{2,1,0:T(8,128)(2,1)S(1)}, bf16[8,16,256]{2,1,0:T(8,128)(2,1)S(1)}, u32[]{:S(2)}, u32[]{:S(2)}) collective-permute-start(bf16[8,16,256]{2,1,0:T(8,128)(2,1)S(1)} %bitcast.131), channel_id=1, source_target_pairs={{0,8},{1,9},{2,10},{3,11},{4,12},{5,13},{6,14},{7,15},{8,0},{9,1},... | collective-permute-start | bytes 196616 | tf_op jit(solution)/shard_map/ppermute | solution.py:21
  16.8 2.9 %collective-permute-start.4 = (bf16[64,8,256]{2,0,1:T(8,128)(2,1)S(1)}, bf16[64,8,256]{2,0,1:T(8,128)(2,1)S(1)}, u32[]{:S(2)}, u32[]{:S(2)}) collective-permute-start(bf16[64,8,256]{2,0,1:T(8,128)(2,1)S(1)} %get-tuple-element.23), channel_id=1, source_target_pairs={{0,1},{1,2},{2,3},{3,4},{4,5},{5,6},{6,7},{7,8},{8,9},{9,10},{10,1... | collective-permute-start | bytes 786440 | tf_op jit(solution)/shard_map/ppermute | solution.py:36
  18.2 5.5 %collective-permute-start.5 = (bf16[64,8,256]{2,0,1:T(8,128)(2,1)S(1)}, bf16[64,8,256]{2,0,1:T(8,128)(2,1)S(1)}, u32[]{:S(2)}, u32[]{:S(2)}) collective-permute-start(bf16[64,8,256]{2,0,1:T(8,128)(2,1)S(1)} %get-tuple-element.24), channel_id=1, source_target_pairs={{1,0},{2,1},{3,2},{4,3},{5,4},{6,5},{7,6},{8,7},{9,8},{10,9},{11,1... | collective-permute-start | bytes 786440 | tf_op jit(solution)/shard_map/ppermute | solution.py:38
  24.0 2.0 %collective-permute-start.6 = (bf16[64,32,8]{2,0,1:T(8,128)(2,1)S(1)}, bf16[64,32,8]{2,0,1:T(8,128)(2,1)S(1)}, u32[]{:S(2)}, u32[]{:S(2)}) collective-permute-start(bf16[64,32,8]{2,0,1:T(8,128)(2,1)S(1)} %get-tuple-element.19), channel_id=1, source_target_pairs={} | collective-permute-start | bytes 98312 | tf_op jit(solution)/shard_map/ppermute | solution.py:36
  24.7 1.3 collective-permute-start.7
  29.0 35.4 %copy-start.4 = (f32[2,64]{1,0:T(2,128)S(1)}, f32[2,64]{1,0:T(2,128)}, u32[]{:S(2)}) copy-start(f32[2,64]{1,0:T(2,128)} %param.14) | copy-start | bytes 1540
  29.7 38.0 %copy-start.3 = (bf16[9,64,64]{2,1,0:T(8,128)(2,1)S(1)}, bf16[9,64,64]{2,1,0:T(8,128)(2,1)}, u32[]{:S(2)}) copy-start(bf16[9,64,64]{2,1,0:T(8,128)(2,1)} %param.13) | copy-start | bytes 221188
  65.1 2.9 %collective-permute-start.8 = (bf16[64,8,256]{2,0,1:T(8,128)(2,1)S(1)}, bf16[64,8,256]{2,0,1:T(8,128)(2,1)S(1)}, u32[]{:S(2)}, u32[]{:S(2)}) collective-permute-start(bf16[64,8,256]{2,0,1:T(8,128)(2,1)S(1)} %get-tuple-element.21), channel_id=1, source_target_pairs={{0,1},{1,2},{2,3},{3,4},{4,5},{5,6},{6,7},{7,8},{8,9},{9,10},{10,1... | collective-permute-start | bytes 786440 | tf_op jit(solution)/shard_map/ppermute | solution.py:36
  66.4 3.4 %collective-permute-start.9 = (bf16[64,8,256]{2,0,1:T(8,128)(2,1)S(1)}, bf16[64,8,256]{2,0,1:T(8,128)(2,1)S(1)}, u32[]{:S(2)}, u32[]{:S(2)}) collective-permute-start(bf16[64,8,256]{2,0,1:T(8,128)(2,1)S(1)} %get-tuple-element.22), channel_id=1, source_target_pairs={{1,0},{2,1},{3,2},{4,3},{5,4},{6,5},{7,6},{8,7},{9,8},{10,9},{11,1... | collective-permute-start | bytes 786440 | tf_op jit(solution)/shard_map/ppermute | solution.py:38
  70.2 1.9 %collective-permute-start.10 = (bf16[64,32,8]{2,0,1:T(8,128)(2,1)S(1)}, bf16[64,32,8]{2,0,1:T(8,128)(2,1)S(1)}, u32[]{:S(2)}, u32[]{:S(2)}) collective-permute-start(bf16[64,32,8]{2,0,1:T(8,128)(2,1)S(1)} %get-tuple-element.15), channel_id=1, source_target_pairs={} | collective-permute-start | bytes 98312 | tf_op jit(solution)/shard_map/ppermute | solution.py:36
  70.9 1.3 collective-permute-start.11
